TPU v7x, 256 devices: a 2x2x32 block of a 4x8x32 slice. The times are simulated.
256 devices in a mesh: beam: 4 (over y, x), freq: 32 (over z), sub: 2 (over core).
Axes of the slice: x: 2, y: 2, z: 32, core: 2. Of those that a mesh axis runs over, the one named last changes fastest.
The devices are a block of a 4x8x32 slice.
Arguments:
- spectrum: bfloat16 [64, 4194304], P('sub', ('beam', 'freq')), parts along dimension 1
- hit_mask: int32 [64, 32768], P('sub', ('beam', 'freq')), parts along dimension 1, may hold values from 0 to 1, as said below
- owner_map: int32 [4096], P(('beam', 'freq')), parts along dimension 0, may hold values from 0 to 1023, as said below
- median_bin: int32 [4096], P(('beam', 'freq')), parts along dimension 0, may hold values from 32 to 559
- mad_bin: int32 [4096], P(('beam', 'freq')), parts along dimension 0, may hold values from 4 to 15
Outputs:
- hit_snr: bfloat16 [32, 2, 16384, 128], P('freq', 'sub', 'beam'), parts along dimension 2
- hit_keys: int32 [32, 2, 16384], P('freq', 'sub', 'beam'), parts along dimension 2
- hit_excess: float32 [32, 2, 16384], P('freq', 'sub', 'beam'), parts along dimension 2
There are 4 independent parts, one for each index of `beam`. A program takes and returns all parts, laid end to end along the dimension named above; each array names one. Nothing has to cross between parts.
Inputs may be any that keep to these rules, and one draw needn't show every extreme that they name: `hit_mask`: for each index of freq, each half of the drift rates and each owner, at most 128 hit blocks go from the first to the last; in every draw some owner gets exactly 128 from every index of freq and half. `owner_map`: A permutation of the slots 0 to 1023; the 32 coarse channels of one index of freq go 1 to each owner, and the slot of index f's coarse channel at each owner is f.
All inputs are finite; a program needn't handle non-finite values.
Results may differ from a plain program's by a relative error of at most 0.007.
Values may be sent and summed in bfloat16 or wider, within the bound.
No kernel may reach another device: no remote copies, remote signals or barrier semaphores. Data moves between devices by JAX's collectives and lax.ppermute only.
A program may use at most 64 MiB of HBM per device.

v0:
```python
import jax
import jax.numpy as jnp
from jax import lax
from jax.sharding import PartitionSpec as P

COARSE_WIDTH = 1024
BLOCK = 128
CAP = 128


BIN_STEP = 0.0625
MAD_WIDTH = 5.0
MAD_SCALE = 1.4826
THRESH = 3.0


def copy_for_each(value, axis):
    devices = lax.axis_size(axis)
    return lax.all_to_all(
        jnp.broadcast_to(value[None], (devices, *value.shape)), axis, 0, 0, tiled=True
    )


def over_copies(value, axis):
    return copy_for_each(value, axis).sum(axis=0)


def together(arrays, axis):
    vector, at, done = (jnp.concatenate([a.reshape(-1) for a in arrays]), 0, [])
    subtotal = over_copies(vector, axis)
    for a in arrays:
        done.append(subtotal[at : at + a.size].reshape(a.shape))
        at += a.size
    return tuple(done)


def pick_from(selector, table):
    return jnp.sum(selector * table[None, :], axis=1)


def per_device(spectrum, hit_mask, owner_map, median_bin, mad_bin):
    drift_dev = spectrum.shape[0]
    coarse_dev = owner_map.shape[0]
    per_coarse = COARSE_WIDTH // BLOCK
    freq_count = lax.axis_size("freq")
    drift_total = drift_dev * lax.axis_size("sub")
    half_index = lax.axis_index("sub")
    slots_total = freq_count * CAP
    power = spectrum.astype(jnp.float32).reshape(drift_dev, coarse_dev, COARSE_WIDTH)
    center = BIN_STEP * median_bin.astype(jnp.float32)
    spread = MAD_WIDTH * BIN_STEP * mad_bin.astype(jnp.float32)
    inside = (power >= (center - spread)[None, :, None]) & (
        power <= (center + spread)[None, :, None]
    )
    kept = jnp.where(inside, power - center[None, :, None], 0.0)
    window_count = jnp.sum(inside.astype(jnp.float32), axis=(0, 2))
    first = jnp.sum(kept, axis=(0, 2))
    second = jnp.sum(kept * kept, axis=(0, 2))
    window_count, first, second = together((window_count, first, second), "sub")
    floor_count = jnp.maximum(window_count, 1.0)
    mean_level = center + first / floor_count
    mad_sigma = MAD_SCALE * BIN_STEP * mad_bin.astype(jnp.float32)
    sigma = jnp.sqrt(0.5 * second / floor_count + 0.5 * mad_sigma * mad_sigma)
    marks = hit_mask.reshape(drift_dev, coarse_dev, per_coarse)
    row_count = jnp.sum(marks, axis=2)
    coarse_count = jnp.sum(row_count, axis=0)
    row_start = jnp.cumsum(row_count, axis=0) - row_count
    dest = owner_map // coarse_dev
    slot_local = owner_map % coarse_dev
    ahead = ((dest[None, :] == dest[:, None]) & (slot_local[None, :] < slot_local[:, None])).astype(
        jnp.int32
    )
    offset = jnp.sum(ahead * coarse_count[None, :], axis=1)
    positions = jnp.arange(slots_total, dtype=jnp.int32)
    target_dest = positions // CAP
    within = positions % CAP
    select = (
        (dest[None, :] == target_dest[:, None])
        & (offset[None, :] <= within[:, None])
        & (within[:, None] < (offset + coarse_count)[None, :])
    )
    filled = jnp.any(select, axis=1)
    pick = select.astype(jnp.int32)
    coarse_ids = jnp.arange(coarse_dev, dtype=jnp.int32)
    chosen_coarse = pick_from(pick, coarse_ids)
    chosen_slot = pick_from(pick, slot_local)
    remain = within - pick_from(pick, offset)
    pick_float = pick.astype(jnp.float32)
    starts_at = jnp.dot(
        pick_float, row_start.T.astype(jnp.float32), precision=lax.Precision.HIGHEST
    ).astype(jnp.int32)
    counts_at = jnp.dot(
        pick_float, row_count.T.astype(jnp.float32), precision=lax.Precision.HIGHEST
    ).astype(jnp.int32)
    row_pick = ((starts_at <= remain[:, None]) & (remain[:, None] < starts_at + counts_at)).astype(
        jnp.int32
    )
    chosen_drift = pick_from(row_pick, jnp.arange(drift_dev, dtype=jnp.int32))
    inner = remain - jnp.sum(row_pick * starts_at, axis=1)
    bit_rows = marks.reshape(-1, per_coarse)[chosen_drift * coarse_dev + chosen_coarse]
    bit_before = jnp.cumsum(bit_rows, axis=1) - bit_rows
    bit_pick = ((bit_rows > 0) & (bit_before == inner[:, None])).astype(jnp.int32)
    chosen_block = pick_from(bit_pick, jnp.arange(per_coarse, dtype=jnp.int32))
    source_row = jnp.where(
        filled, (chosen_drift * coarse_dev + chosen_coarse) * per_coarse + chosen_block, 0
    )
    slot_keys = jnp.where(
        filled,
        (chosen_slot * drift_total + half_index * drift_dev + chosen_drift) * per_coarse
        + chosen_block,
        -1,
    )
    blocks = spectrum.reshape(-1, BLOCK)[source_row]
    level = jnp.sum(pick_float * mean_level[None, :], axis=1)
    scale = jnp.where(filled, jnp.sum(pick_float * sigma[None, :], axis=1), 1.0)
    normal = (blocks.astype(jnp.float32) - level[:, None]) / scale[:, None]
    payload = jnp.where(filled[:, None], normal, 0.0).astype(jnp.bfloat16)
    arrived = lax.all_to_all(
        payload.reshape(freq_count, CAP, BLOCK), "freq", split_axis=0, concat_axis=0, tiled=True
    )
    keys = lax.all_to_all(
        slot_keys.reshape(freq_count, CAP), "freq", split_axis=0, concat_axis=0, tiled=True
    )
    excess = jnp.sum(jnp.maximum(arrived.astype(jnp.float32) - THRESH, 0.0), axis=-1)
    hit_rows, arrived_keys, excess = (arrived, keys, excess)
    got = jnp.sum((arrived_keys >= 0).astype(jnp.int32), axis=1)
    ends = jnp.cumsum(got)
    begins = ends - got
    source_of = jnp.sum((ends[None, :] <= positions[:, None]).astype(jnp.int32), axis=1)
    live = source_of < freq_count
    source_clip = jnp.minimum(source_of, freq_count - 1)
    source_hot = (jnp.arange(freq_count, dtype=jnp.int32)[None, :] == source_clip[:, None]).astype(
        jnp.int32
    )
    begin_of = jnp.sum(source_hot * begins[None, :], axis=1)
    take = jnp.where(live, source_clip * CAP + positions - begin_of, 0)
    hit_snr = jnp.where(
        live[:, None], hit_rows.reshape(-1, BLOCK)[take], jnp.zeros((1, BLOCK), jnp.bfloat16)
    )
    hit_keys = jnp.where(live, arrived_keys.reshape(-1)[take], -1).astype(jnp.int32)
    hit_excess = jnp.where(live, excess.reshape(-1)[take], 0.0)
    return (
        hit_snr.reshape(1, 1, slots_total, BLOCK),
        hit_keys.reshape(1, 1, slots_total),
        hit_excess.reshape(1, 1, slots_total),
    )


def solution(mesh):
    placed = (
        P("sub", ("beam", "freq")),
        P("sub", ("beam", "freq")),
        P(("beam", "freq")),
        P(("beam", "freq")),
        P(("beam", "freq")),
    )
    return jax.shard_map(
        per_device,
        mesh=mesh,
        in_specs=placed,
        out_specs=(
            P("freq", "sub", "beam", None),
            P("freq", "sub", "beam"),
            P("freq", "sub", "beam"),
        ),
        check_vma=False,
    )
```

profile of v0, /device:TPU:46, one launch (start us, length us, event | category | flops | bytes accessed | tf_op | source)
XLA Modules:
  0.0 246.0 jit_solution(17346366266765123883)
XLA Ops:
  0.6 0.7 fusion.28
  1.3 0.1 broadcast_bitcast_fusion.2
  1.4 0.1 broadcast_bitcast_fusion
  1.6 3.6 %fusion.5 = (f32[32768]{0:T(1024)S(1)}, f32[32768]{0:T(1024)S(1)}, f32[32768]{0:T(1024)S(1)}) fusion(bf16[32,32768]{1,0:T(8,128)(2,1)} %param.5, f32[32768]{0:T(1024)S(1)} %bitcast.42, f32[32768]{0:T(1024)S(1)} %bitcast.43, f32[32768]{0:T(1024)S(1)} %bitcast.41), kind=kLoop, calls=%fused_computation.15 | loop fusion | flops 11436032 | bytes 2883584 | tf_op jit(solution)/shard_map/reduce_sum | solution.py:57
  5.3 0.1 reduce_sum.227
  5.5 0.1 reduce_sum.230
  5.6 0.1 reduce_sum.224
  5.7 0.1 pad_maximum_fusion
  5.8 0.6 broadcast_in_dim.49
  6.4 3.2 %all-to-all-start.1 = ((f32[2,1,96]{2,1,0:T(1,128)}), f32[2,1,96]{2,1,0:T(1,128)S(1)}, u32[]{:S(2)}, u32[]{:S(2)}) async-start(f32[2,1,96]{2,1,0:T(1,128)} %broadcast_in_dim.49), calls=%async_computation.1 | async-start | bytes 2048 | tf_op jit(solution)/shard_map/all_to_all | solution.py:19
  9.6 0.1 copy.25
  9.8 0.1 reduce_sum.208
  9.9 0.1 reduce_sum.209
  10.0 0.2 select_reduce_fusion.7
  10.2 0.7 all-to-all-done.1
  10.9 0.1 add_sqrt_fusion
  11.0 0.3 multiply_reduce_fusion.1
  11.3 0.3 select_reduce_fusion.6
  11.7 0.3 reshape_reshape.3
  12.0 0.1 copy.26
  12.1 0.1 reduce_window_sum.29
  12.2 0.6 convolution_convert_fusion.1
  12.8 0.8 select_reduce_fusion.2
  13.7 10.8 %gather_fusion = s32[4096,8]{1,0:T(8,128)S(1)} fusion(s32[1024,8]{1,0:T(8,128)S(1)} %reshape_reshape.3, s32[4096]{0:T(1024)S(1)} %broadcast_clamp_fusion.2), kind=kCustom, calls=%fused_computation | custom fusion | bytes 278528 | tf_op jit(solution)/shard_map/gather | solution.py:100
  24.5 2.4 reduce_window_sum.30
  26.9 0.1 reduce_or.13
  27.0 2.5 %select_reduce_fusion = s32[4096]{0:T(1024)S(1)} fusion(s32[4096,8]{1,0:T(8,128)} %reduce_window_sum.30, s32[4096,8]{1,0:T(8,128)S(1)} %gather_fusion, s32[4096]{0:T(1024)S(1)} %fusion.29), kind=kLoop, calls=%fused_computation.24 | loop fusion | flops 192512 | bytes 294912 | tf_op jit(solution)/shard_map/reduce_sum | solution.py:38
  29.5 0.6 add_select_fusion.1
  30.1 32.7 %all-to-all-start = ((s32[32,1,128]{2,1,0:T(1,128)}), s32[32,1,128]{2,1,0:T(1,128)S(1)}, u32[]{:S(2)}, u32[]{:S(2)}) async-start(s32[32,1,128]{2,1,0:T(1,128)} %bitcast.3), calls=%async_computation | async-start | bytes 32768 | tf_op jit(solution)/shard_map/all_to_all | solution.py:121
  62.8 2.9 %reshape.382 = bf16[8192,128]{1,0:T(8,128)(2,1)S(1)} reshape(bf16[32,32768]{1,0:T(8,128)(2,1)} %param.5) | data formatting | bytes 4194304 | tf_op jit(solution)/shard_map/reshape | solution.py:113
  65.8 12.1 %gather_fusion.1 = bf16[4096,128]{1,0:T(8,128)(2,1)S(1)} fusion(bf16[8192,128]{1,0:T(8,128)(2,1)S(1)} %reshape.382, s32[4096]{0:T(1024)S(1)} %broadcast_clamp_fusion.1), kind=kCustom, calls=%fused_computation.1 | custom fusion | bytes 2113536 | tf_op jit(solution)/shard_map/gather | solution.py:113
  77.9 2.9 %fusion.10 = bf16[32,128,128]{2,1,0:T(8,128)(2,1)} fusion(bf16[32,128,128]{2,1,0:T(8,128)(2,1)S(1)} %bitcast.40, f32[32,128]{1,0:T(8,128)S(1)} %bitcast_select_fusion.1, f32[32,128]{1,0:T(8,128)S(1)} %bitcast.48, pred[32,128]{1,0:T(8,128)(4,1)S(1)} %bitcast.47), kind=kLoop, calls=%fused_computation.22 | loop fusion | flops 2621440 | bytes 2134016 | tf_op jit(solution)/shard_map/convert_element_type | solution.py:117
  80.7 3.7 %all-to-all-done = s32[32,1,128]{2,1,0:T(1,128)S(1)} async-done(((s32[32,1,128]{2,1,0:T(1,128)}), s32[32,1,128]{2,1,0:T(1,128)S(1)}, u32[]{:S(2)}, u32[]{:S(2)}) %all-to-all-start) | async-done | bytes 16416 | tf_op jit(solution)/shard_map/all_to_all | solution.py:121
  84.5 18.5 %all-to-all-start.2 = ((bf16[32,128,128]{2,1,0:T(8,128)(2,1)}), bf16[32,128,128]{2,1,0:T(8,128)(2,1)S(1)}, u32[]{:S(2)}, u32[]{:S(2)}) async-start(bf16[32,128,128]{2,1,0:T(8,128)(2,1)} %fusion.10), calls=%async_computation.2 | async-start | bytes 2097152 | tf_op jit(solution)/shard_map/all_to_all | solution.py:118
  103.0 0.1 convert_reduce_fusion.2
  103.1 0.1 copy.29
  103.2 0.1 reduce-window.7
  103.2 0.1 reduce.11
  103.3 0.1 convert_reduce_fusion.1
  103.5 0.2 select_reduce_fusion.1
  103.8 23.0 %gather_fusion.3 = s32[4096]{0:T(1024)S(1)} fusion(s32[4096]{0:T(1024)S(1)} %bitcast.37, s32[4096]{0:T(1024)S(1)} %broadcast_clamp_fusion), kind=kCustom, calls=%fused_computation.3 | custom fusion | bytes 49152 | tf_op jit(solution)/shard_map/gather | solution.py:140
  126.8 0.6 broadcast_select_fusion.1
  127.4 79.4 %all-to-all-done.2 = bf16[32,128,128]{2,1,0:T(8,128)(2,1)S(1)} async-done(((bf16[32,128,128]{2,1,0:T(8,128)(2,1)}), bf16[32,128,128]{2,1,0:T(8,128)(2,1)S(1)}, u32[]{:S(2)}, u32[]{:S(2)}) %all-to-all-start.2) | async-done | bytes 1048608 | tf_op jit(solution)/shard_map/all_to_all | solution.py:118
  206.8 0.6 maximum_reduce_fusion
  207.4 23.0 %gather_fusion.4 = f32[4096]{0:T(1024)S(1)} fusion(f32[4096]{0:T(1024)S(1)} %bitcast.38, s32[4096]{0:T(1024)S(1)} %broadcast_clamp_fusion), kind=kCustom, calls=%fused_computation.4 | custom fusion | bytes 49152 | tf_op jit(solution)/shard_map/gather | solution.py:141
  230.4 12.1 %gather_fusion.2 = bf16[4096,128]{1,0:T(8,128)(2,1)S(1)} fusion(bf16[4096,128]{1,0:T(8,128)(2,1)S(1)} %bitcast.39, s32[4096]{0:T(1024)S(1)} %broadcast_clamp_fusion), kind=kCustom, calls=%fused_computation.2 | custom fusion | bytes 2113536 | tf_op jit(solution)/shard_map/gather | solution.py:138
  242.6 0.6 broadcast_select_fusion
  243.2 2.9 %bitcast_select_fusion = bf16[1,1,4096,128]{3,2,1,0:T(8,128)(2,1)} fusion(bf16[4096,128]{1,0:T(8,128)(2,1)S(1)} %gather_fusion.2, pred[4096]{0:T(1024)(128)(4,1)S(1)} %broadcast_compare_fusion), kind=kLoop, calls=%fused_computation.27 | loop fusion | flops 524288 | bytes 2101248 | tf_op jit(solution)/shard_map/jit(_where)/select_n | solution.py:137
  (34 shorter events, 0.5 us)
Async XLA Ops:
  1.6 8.1 %copy-start = (s32[32,256]{1,0:T(8,128)S(1)}, s32[32,256]{1,0:T(8,128)}, u32[]{:S(2)}) copy-start(s32[32,256]{1,0:T(8,128)} %param.6) | copy-start | bytes 98308
  1.6 8.2 %copy-start.3 = (s32[32]{0:T(128)S(1)}, s32[32]{0:T(128)}, u32[]{:S(2)}) copy-start(s32[32]{0:T(128)} %param.7) | copy-start | bytes 388
  1.6 9.3 %copy-start.1 = (s32[32]{0:T(128)S(1)}, s32[32]{0:T(128)}, u32[]{:S(2)}) copy-start(s32[32]{0:T(128)} %param.9) | copy-start | bytes 388
  1.6 9.3 %copy-start.2 = (s32[32]{0:T(128)S(1)}, s32[32]{0:T(128)}, u32[]{:S(2)}) copy-start(s32[32]{0:T(128)} %param.8) | copy-start | bytes 388
  6.4 4.5 %all-to-all-start.1 = ((f32[2,1,96]{2,1,0:T(1,128)}), f32[2,1,96]{2,1,0:T(1,128)S(1)}, u32[]{:S(2)}, u32[]{:S(2)}) async-start(f32[2,1,96]{2,1,0:T(1,128)} %broadcast_in_dim.49), calls=%async_computation.1 | async-start | bytes 2048 | tf_op jit(solution)/shard_map/all_to_all | solution.py:19
  30.1 54.4 %all-to-all-start = ((s32[32,1,128]{2,1,0:T(1,128)}), s32[32,1,128]{2,1,0:T(1,128)S(1)}, u32[]{:S(2)}, u32[]{:S(2)}) async-start(s32[32,1,128]{2,1,0:T(1,128)} %bitcast.3), calls=%async_computation | async-start | bytes 32768 | tf_op jit(solution)/shard_map/all_to_all | solution.py:121
  84.5 122.3 %all-to-all-start.2 = ((bf16[32,128,128]{2,1,0:T(8,128)(2,1)}), bf16[32,128,128]{2,1,0:T(8,128)(2,1)S(1)}, u32[]{:S(2)}, u32[]{:S(2)}) async-start(bf16[32,128,128]{2,1,0:T(8,128)(2,1)} %fusion.10), calls=%async_computation.2 | async-start | bytes 2097152 | tf_op jit(solution)/shard_map/all_to_all | solution.py:118
where the time goes:
time: 247 us; the launch traced here: 246 us
  local copies, waits for them, and re-layouts  85.6 us (35%)
  waiting for transfers between devices  83.8 us (34%)
  starting transfers between devices  54.4 us (22%)
  other arithmetic  19.8 us (8%)
    all_to_all x1, waiting for transfers between devices, per_device(): lax.all_to_all(payload.reshape(freq_count, CAP, BLOCK), 'freq', split_axi...  79.4 us
    all_to_all x1, starting transfers between devices, per_device(): lax.all_to_all(slot_keys.reshape(freq_count, CAP), 'freq', split_axis=0,...  32.7 us
    gather x1, local copies, waits for them, and re-layouts, per_device(): arrived_keys.reshape(-1)[take]  23 us
    gather x1, local copies, waits for them, and re-layouts, per_device(): hit_excess = jnp.where(live, excess.reshape(-1)[take], 0.0)  23 us
    all_to_all x1, starting transfers between devices, per_device(): lax.all_to_all(payload.reshape(freq_count, CAP, BLOCK), 'freq', split_axi...  18.5 us
    gather x1, local copies, waits for them, and re-layouts, per_device(): hit_rows.reshape(-1, BLOCK)[take]  12.1 us
    gather x1, local copies, waits for them, and re-layouts, per_device(): blocks = spectrum.reshape(-1, BLOCK)[source_row]  12.1 us
    gather x1, local copies, waits for them, and re-layouts, per_device(): marks.reshape(-1, per_coarse)[chosen_drift * coarse_dev + chosen_coarse]  10.8 us
  transfers between devices with their start and end apart: 3, of which 3 were waited for; matrix products, arithmetic and copies ran while one was open for 17% of the time, Pallas kernels for 0%

commit v1 on v0

v1 whole, which is shorter than its diff:
```python
import functools

import jax
import jax.numpy as jnp
from jax import lax
from jax.experimental import pallas as pl
from jax.experimental.pallas import tpu as pltpu
from jax.sharding import PartitionSpec as P

COARSE_WIDTH = 1024
BLOCK = 128
CAP = 128
PER_COARSE = COARSE_WIDTH // BLOCK

BIN_STEP = 0.0625
MAD_WIDTH = 5.0
MAD_SCALE = 1.4826
THRESH = 3.0
LIMIT = 16 * 1024 * 1024

F32 = jnp.float32
BF16 = jnp.bfloat16


def iota(shape, axis):
    return lax.broadcasted_iota(jnp.int32, shape, axis)


def dot(a, b, dims=((1,), (0,))):
    return lax.dot_general(a, b, (dims, ((), ())), preferred_element_type=F32)


def pack_kernel(drifts, coarse, group, map_ref, mask_ref, spec_ref, out_ref, key_ref, rank_ref):
    step = pl.program_id(0)
    width = PER_COARSE * drifts

    @pl.when(step == 0)
    def _():
        marks = mask_ref[...].astype(F32).astype(BF16)
        row = jnp.zeros((coarse, width), F32)
        for b in range(PER_COARSE):
            pick = iota((coarse * PER_COARSE, coarse), 0) == iota(
                (coarse * PER_COARSE, coarse), 1
            ) * PER_COARSE + b
            of_block = dot(marks, jnp.where(pick, 1.0, 0.0).astype(BF16))
            place = iota((drifts, width), 1) == iota((drifts, width), 0) + b * drifts
            row += dot(
                of_block.astype(BF16), jnp.where(place, 1.0, 0.0).astype(BF16), ((0,), (0,))
            )
        order = lambda k: (k % drifts) * PER_COARSE + k // drifts
        before = order(iota((width, width), 0)) < order(iota((width, width), 1))
        rank = dot(row.astype(BF16), jnp.where(before, 1.0, 0.0).astype(BF16))
        rank_ref[...] = jnp.where(row > 0.5, rank, -1.0)

    slots = iota((CAP, width), 0).astype(F32)
    position = iota((width, CAP), 0)
    label = ((position % drifts) * PER_COARSE + position // drifts + 1).astype(F32).astype(BF16)
    diagonal = iota((CAP, CAP), 0) == iota((CAP, CAP), 1)
    for j in range(group):
        at = step * group + j
        owner = lax.div(map_ref[at], coarse)
        chosen = jnp.where(rank_ref[pl.ds(at, 1), :] == slots, 1.0, 0.0).astype(BF16)
        base = j * COARSE_WIDTH
        rows = jnp.concatenate(
            [spec_ref[:, base + b * BLOCK : base + (b + 1) * BLOCK] for b in range(PER_COARSE)],
            axis=0,
        )
        taken = dot(chosen, jnp.concatenate([rows, label], axis=1))
        out_ref[owner] = taken[:, :BLOCK].astype(BF16)
        key_ref[pl.ds(owner, 1), :] = jnp.sum(
            jnp.where(diagonal, taken[:, BLOCK:], 0.0), axis=0, keepdims=True
        )


def pack(spectrum, hit_mask, owner_map):
    drifts, channels = spectrum.shape
    coarse = owner_map.shape[0]
    group = 8
    return pl.pallas_call(
        functools.partial(pack_kernel, drifts, coarse, group),
        out_shape=(
            jax.ShapeDtypeStruct((coarse, CAP, BLOCK), BF16),
            jax.ShapeDtypeStruct((coarse, CAP), F32),
        ),
        grid_spec=pltpu.PrefetchScalarGridSpec(
            num_scalar_prefetch=1,
            grid=(coarse // group,),
            in_specs=[
                pl.BlockSpec((drifts, coarse * PER_COARSE), lambda i, m: (0, 0)),
                pl.BlockSpec((drifts, group * COARSE_WIDTH), lambda i, m: (0, i)),
            ],
            out_specs=[
                pl.BlockSpec((coarse, CAP, BLOCK), lambda i, m: (0, 0, 0)),
                pl.BlockSpec((coarse, CAP), lambda i, m: (0, 0)),
            ],
            scratch_shapes=[pltpu.VMEM((coarse, PER_COARSE * drifts), F32)],
        ),
        compiler_params=pltpu.CompilerParams(vmem_limit_bytes=LIMIT),
        name="pack",
    )(owner_map, hit_mask, spectrum)


def unpack_kernel(senders, steps, at_ref, meta_ref, rows_ref, snr_ref, key_ref, excess_ref, list_ref, keys_ref):
    step = pl.program_id(0)
    total = at_ref[senders]

    @pl.when(step == 0)
    def _():
        lane = iota((1, CAP), 1)
        half = at_ref[senders + 1]
        for f in range(senders):
            start = at_ref[f]
            stats = meta_ref[f, 1:2, :]
            raw = rows_ref[f].astype(F32)
            list_ref[pl.ds(start, CAP), :] = (raw - stats[:, 0:1]) * stats[:, 1:2]
            key = meta_ref[f, 0:1, :].astype(jnp.int32) + (f * 512 + half * 256 - 1)
            row = lax.div(start, CAP)
            shift = lax.rem(start, CAP)
            moved = pltpu.roll(key, shift, 1)
            keys_ref[pl.ds(row, 1), :] = jnp.where(
                lane >= shift, moved, keys_ref[pl.ds(row, 1), :]
            )
            keys_ref[pl.ds(row + 1, 1), :] = moved

    per = senders // steps
    ones = jnp.ones((2 * BLOCK, BLOCK), BF16)
    diagonal = iota((CAP, CAP), 0) == iota((CAP, CAP), 1)
    for j in range(per):
        row = step * per + j
        first = row * CAP
        block = list_ref[pl.ds(pl.multiple_of(first, CAP), CAP), :]
        live = iota((CAP, BLOCK), 0) + first < total
        value = jnp.where(live, block, 0.0).astype(BF16)
        snr_ref[0, 0, j * CAP : (j + 1) * CAP, :] = value
        over = jnp.maximum(value.astype(F32) - THRESH, 0.0)
        high = over.astype(BF16)
        low = (over - high.astype(F32)).astype(BF16)
        sums = dot(jnp.concatenate([high, low], axis=1), ones)
        excess_ref[pl.ds(row, 1), :] = jnp.sum(
            jnp.where(diagonal, sums, 0.0), axis=0, keepdims=True
        )
        key_ref[pl.ds(row, 1), :] = jnp.where(
            iota((1, CAP), 1) + first < total, keys_ref[pl.ds(row, 1), :], -1
        )


def unpack(at, meta, arrived):
    senders = arrived.shape[0]
    steps = 4
    total = senders * CAP
    return pl.pallas_call(
        functools.partial(unpack_kernel, senders, steps),
        out_shape=(
            jax.ShapeDtypeStruct((1, 1, total, BLOCK), BF16),
            jax.ShapeDtypeStruct((senders, CAP), jnp.int32),
            jax.ShapeDtypeStruct((senders, CAP), F32),
        ),
        grid_spec=pltpu.PrefetchScalarGridSpec(
            num_scalar_prefetch=1,
            grid=(steps,),
            in_specs=[
                pl.BlockSpec((senders, 2, CAP), lambda i, m: (0, 0, 0)),
                pl.BlockSpec((senders, CAP, BLOCK), lambda i, m: (0, 0, 0)),
            ],
            out_specs=[
                pl.BlockSpec((1, 1, total // steps, BLOCK), lambda i, m: (0, 0, i, 0)),
                pl.BlockSpec((senders, CAP), lambda i, m: (0, 0)),
                pl.BlockSpec((senders, CAP), lambda i, m: (0, 0)),
            ],
            scratch_shapes=[
                pltpu.VMEM((total, BLOCK), F32),
                pltpu.VMEM((senders + 8, CAP), jnp.int32),
            ],
        ),
        compiler_params=pltpu.CompilerParams(vmem_limit_bytes=LIMIT),
        name="unpack",
    )(at, meta, arrived)


def statistics(spectrum, median_bin, mad_bin):
    drifts = spectrum.shape[0]
    coarse = median_bin.shape[0]
    power = spectrum.astype(F32).reshape(drifts, coarse, COARSE_WIDTH)
    center = BIN_STEP * median_bin.astype(F32)
    spread = MAD_WIDTH * BIN_STEP * mad_bin.astype(F32)
    inside = (power >= (center - spread)[None, :, None]) & (
        power <= (center + spread)[None, :, None]
    )
    kept = jnp.where(inside, power - center[None, :, None], 0.0)
    count = jnp.sum(inside.astype(F32), axis=(0, 2))
    first = jnp.sum(kept, axis=(0, 2))
    second = jnp.sum(kept * kept, axis=(0, 2))
    mine = jnp.stack([count, first, second])
    pairs = lax.axis_size("sub")
    total = mine
    for k in range(1, pairs):
        total = total + lax.ppermute(mine, "sub", [(i, (i + k) % pairs) for i in range(pairs)])
    count, first, second = total[0], total[1], total[2]
    floor_count = jnp.maximum(count, 1.0)
    mean_level = center + first / floor_count
    mad_sigma = MAD_SCALE * BIN_STEP * mad_bin.astype(F32)
    sigma = jnp.sqrt(0.5 * second / floor_count + 0.5 * mad_sigma * mad_sigma)
    return mean_level, 1.0 / sigma


def per_device(spectrum, hit_mask, owner_map, median_bin, mad_bin):
    coarse = owner_map.shape[0]
    senders = lax.axis_size("freq")
    payload, labels = pack(spectrum, hit_mask, owner_map)
    spectrum, payload = lax.optimization_barrier((spectrum, payload))
    with jax.named_scope("payload"):
        arrived = lax.all_to_all(payload, "freq", 0, 0, tiled=True)
    mean_level, inverse = statistics(spectrum, median_bin, mad_bin)
    owner = owner_map // coarse
    mine = owner[None, :] == jnp.arange(senders, dtype=jnp.int32)[:, None]
    level_to = jnp.sum(jnp.where(mine, mean_level[None, :], 0.0), axis=1)
    inverse_to = jnp.sum(jnp.where(mine, inverse[None, :], 0.0), axis=1)
    lane = jnp.arange(CAP, dtype=jnp.int32)[None, :]
    stats = jnp.where(lane == 0, level_to[:, None], inverse_to[:, None])
    with jax.named_scope("meta"):
        meta = lax.all_to_all(jnp.stack([labels, stats], axis=1), "freq", 0, 0, tiled=True)
    got = jnp.sum((meta[:, 0, :] > 0.5).astype(jnp.int32), axis=1)
    rank = jnp.arange(senders, dtype=jnp.int32)
    starts = jnp.sum(jnp.where(rank[None, :] < rank[:, None], got[None, :], 0), axis=1)
    at = jnp.concatenate(
        [starts, jnp.sum(got)[None], lax.axis_index("sub").astype(jnp.int32)[None]]
    )
    snr, keys, excess = unpack(at, meta, arrived)
    total = senders * CAP
    return snr, keys.reshape(1, 1, total), excess.reshape(1, 1, total)


def solution(mesh):
    placed = (
        P("sub", ("beam", "freq")),
        P("sub", ("beam", "freq")),
        P(("beam", "freq")),
        P(("beam", "freq")),
        P(("beam", "freq")),
    )
    return jax.shard_map(
        per_device,
        mesh=mesh,
        in_specs=placed,
        out_specs=(
            P("freq", "sub", "beam", None),
            P("freq", "sub", "beam"),
            P("freq", "sub", "beam"),
        ),
        check_vma=False,
    )
```

time: 247 us -> 185 us (0.75)
  local copies, waits for them, and re-layouts: 85.6 us -> 3.34 us
  blocking collectives: 0 us -> 55.2 us
  starting transfers between devices: 54.4 us -> 4.99 us
  waiting for transfers between devices: 83.8 us -> 107 us
  other arithmetic: 19.8 us -> 5.45 us
  Pallas kernels: 0 us -> 7.61 us
    gather x5 -> x0, local copies, waits for them, and re-layouts: 81.1 us -> none  [the longest x1 23 us: per_device(): arrived_keys.reshape(-1)[take]]
    all_to_all x0 -> x1, blocking collectives: none -> 55.2 us  [per_device(): lax.all_to_all(jnp.stack([labels, stats], axis=1), 'freq', 0, 0, tiled=True)]
    all_to_all x3 -> x1, starting transfers between devices: 54.4 us -> 4.85 us  [per_device(): arrived = lax.all_to_all(payload, 'freq', 0, 0, tiled=True)]
    all_to_all x3 -> x1, waiting for transfers between devices: 83.8 us -> 106 us  [per_device(): arrived = lax.all_to_all(payload, 'freq', 0, 0, tiled=True)]
    pallas_call x0 -> x2, Pallas kernels: none -> 7.61 us  [the longest x1 4.43 us: pack(): pl.pallas_call(functools.partial(pack_kernel, drifts, coarse, group), out...]
    reduce_sum x16 -> x7, other arithmetic: 8.49 us -> 3.82 us  [the longest x2 2.15 us: statistics(): first = jnp.sum(kept, axis=(0, 2))]
    select_n x10 -> x2, other arithmetic: 4.82 us -> 0.15 us  [the longest x1 0.14 us: per_device(): stats = jnp.where(lane == 0, level_to[:, None], inverse_to[:, None])]
    reshape x1 -> x0, local copies, waits for them, and re-layouts: 2.88 us -> none  [per_device(): blocks = spectrum.reshape(-1, BLOCK)[source_row]]
  transfers between devices with their start and end apart: 3 -> 2, of which waited for: 3 -> 2; matrix products, arithmetic and copies ran while one was open for 17% -> 1% of each run, Pallas kernels for 0% -> 0%
where the time goes in v1:
time: 185 us
  waiting for transfers between devices  107 us (58%)
  blocking collectives  55.2 us (30%)
  Pallas kernels  7.61 us (4%)
  other arithmetic  5.45 us (3%)
  starting transfers between devices  4.99 us (3%)
  local copies, waits for them, and re-layouts  3.34 us (2%)
    all_to_all x1, waiting for transfers between devices, per_device(): arrived = lax.all_to_all(payload, 'freq', 0, 0, tiled=True)  106 us
    all_to_all x1, blocking collectives, per_device(): lax.all_to_all(jnp.stack([labels, stats], axis=1), 'freq', 0, 0, tiled=True)  55.2 us
    all_to_all x1, starting transfers between devices, per_device(): arrived = lax.all_to_all(payload, 'freq', 0, 0, tiled=True)  4.85 us
    pallas_call x1, Pallas kernels, pack(): pl.pallas_call(functools.partial(pack_kernel, drifts, coarse, group), out...  4.43 us
  transfers between devices with their start and end apart: 2, of which 2 were waited for; matrix products, arithmetic and copies ran while one was open for 1% of the time, Pallas kernels for 0%

profile of v1, /device:TPU:46, one launch (start us, length us, event | category | flops | bytes accessed | tf_op | source)
XLA Modules:
  0.0 184.8 jit_solution(4199047063475379158)
XLA Ops:
  0.6 0.7 fusion.9
  1.3 0.1 broadcast_bitcast_fusion
  1.5 0.0 copy-start
  1.5 1.6 copy-done
  3.1 0.0 copy-start.2
  3.1 0.8 copy-done.2
  3.8 0.0 copy-start.3
  3.8 0.7 copy-done.3
  4.5 0.0 copy-start.1
  4.5 4.4 %pack.1 = (bf16[32,128,128]{2,1,0:T(8,128)(2,1)}, f32[32,128]{1,0:T(8,128)S(1)}) custom-call(s32[32]{0:T(128)S(1)} %copy-done.3, s32[32,256]{1,0:T(8,128)S(1)} %copy-done.2, bf16[32,32768]{1,0:T(8,128)(2,1)S(1)} %copy-done), custom_call_target="tpu_custom_call" | custom-call | tf_op jit(solution)/shard_map/pack/pallas_call | solution.py:79
  8.9 0.1 broadcast_bitcast_fusion.2
  9.0 0.0 copy-start.4
  9.0 0.0 copy-start.5
  9.0 0.0 copy-start.6
  9.1 0.0 copy-done.1
  9.1 2.0 %fusion.2 = (f32[32768]{0:T(1024)S(1)}, f32[32768]{0:T(1024)S(1)}, f32[32768]{0:T(1024)S(1)}) fusion(bf16[32,32768]{1,0:T(8,128)(2,1)S(1)} %copy-done.1, f32[32768]{0:T(1024)S(1)} %bitcast.25, f32[32768]{0:T(1024)S(1)} %bitcast.24, f32[32768]{0:T(1024)S(1)} %bitcast.26), kind=kLoop, calls=%fused_computation.5 | loop fusion | flops 11436032 | bytes 2883584 | tf_op jit(solution)/shard_map/reduce_sum | solution.py:191
  11.2 0.1 reduce_sum.95
  11.3 0.1 reduce_sum.98
  11.4 0.1 reduce_sum.101
  11.6 0.1 collective-permute-start
  11.7 0.0 copy-done.4
  11.8 1.1 collective-permute-done
  12.9 0.0 copy-done.5
  12.9 0.0 copy-done.6
  12.9 0.1 select_reduce_fusion.2
  13.0 0.1 broadcast_select_fusion
  13.2 55.2 %all_to_all.10.meta_ref = f32[32,2,128]{2,1,0:T(2,128)S(1)} all-to-all(f32[32,2,128]{2,1,0:T(2,128)S(1)} %pad_maximum_fusion), channel_id=1, replica_groups=mesh['beam'=4,'freq'=32,'sub'=2] {'freq'}, dimensions={0} | all-to-all | bytes 65536 | tf_op jit(solution)/shard_map/meta/all_to_all | solution.py:221
  68.4 4.8 %all-to-all-start.1 = ((bf16[32,128,128]{2,1,0:T(8,128)(2,1)}), bf16[32,128,128]{2,1,0:T(8,128)(2,1)S(1)}, u32[]{:S(2)}, u32[]{:S(2)}) async-start(bf16[32,128,128]{2,1,0:T(8,128)(2,1)} %get-tuple-element.13), calls=%async_computation.1 | async-start | bytes 2097152 | tf_op jit(solution)/shard_map/payload/all_to_all | solution.py:212
  73.3 1.2 fusion.6
  74.5 0.1 select_reduce_fusion
  74.6 0.7 pad_add_fusion.at_ref
  75.3 106.3 %all-to-all-done.1.rows_ref = bf16[32,128,128]{2,1,0:T(8,128)(2,1)S(1)} async-done(((bf16[32,128,128]{2,1,0:T(8,128)(2,1)}), bf16[32,128,128]{2,1,0:T(8,128)(2,1)S(1)}, u32[]{:S(2)}, u32[]{:S(2)}) %all-to-all-start.1) | async-done | bytes 1048608 | tf_op jit(solution)/shard_map/payload/all_to_all | solution.py:212
  181.6 3.2 %unpack.1 = (bf16[1,1,4096,128]{3,2,1,0:T(8,128)(2,1)}, s32[32,128]{1,0:T(8,128)}, f32[32,128]{1,0:T(8,128)}) custom-call(s32[34]{0:T(128)S(1)} %pad_add_fusion.at_ref, f32[32,2,128]{2,1,0:T(2,128)S(1)} %all_to_all.10.meta_ref, bf16[32,128,128]{2,1,0:T(8,128)(2,1)S(1)} %all-to-all-done.1.rows_ref), custom_call_target="tpu_custom_call" | custom-call | tf_op jit(solution)/shard_map/unpack/pallas_call | solution.py:151
  (12 shorter events, 0.2 us)
Async XLA Ops:
  1.5 1.6 copy-start
  3.1 0.8 copy-start.2
  3.8 0.7 copy-start.3
  4.5 4.6 %copy-start.1 = (bf16[32,32768]{1,0:T(8,128)(2,1)S(1)}, bf16[32,32768]{1,0:T(8,128)(2,1)}, u32[]{:S(2)}) copy-start(bf16[32,32768]{1,0:T(8,128)(2,1)} %spec_ref.1) | copy-start | bytes 6291460
  9.0 2.7 %copy-start.4 = (s32[32]{0:T(128)S(1)}, s32[32]{0:T(128)}, u32[]{:S(2)}) copy-start(s32[32]{0:T(128)} %map_ref.1) | copy-start | bytes 388
  9.0 3.8 %copy-start.5 = (s32[32]{0:T(128)S(1)}, s32[32]{0:T(128)}, u32[]{:S(2)}) copy-start(s32[32]{0:T(128)} %param.9) | copy-start | bytes 388
  9.0 3.8 %copy-start.6 = (s32[32]{0:T(128)S(1)}, s32[32]{0:T(128)}, u32[]{:S(2)}) copy-start(s32[32]{0:T(128)} %param.8) | copy-start | bytes 388
  11.6 1.3 collective-permute-start
  68.4 113.2 %all-to-all-start.1 = ((bf16[32,128,128]{2,1,0:T(8,128)(2,1)}), bf16[32,128,128]{2,1,0:T(8,128)(2,1)S(1)}, u32[]{:S(2)}, u32[]{:S(2)}) async-start(bf16[32,128,128]{2,1,0:T(8,128)(2,1)} %get-tuple-element.13), calls=%async_computation.1 | async-start | bytes 2097152 | tf_op jit(solution)/shard_map/payload/all_to_all | solution.py:212

commit v2 on v1

v2 whole, which is shorter than its diff:
```python
import functools

import jax
import jax.numpy as jnp
from jax import lax
from jax.experimental import pallas as pl
from jax.experimental.pallas import tpu as pltpu
from jax.sharding import PartitionSpec as P

COARSE_WIDTH = 1024
BLOCK = 128
CAP = 128
PER_COARSE = COARSE_WIDTH // BLOCK
EXTRA = 8
ROWS = CAP + EXTRA

BIN_STEP = 0.0625
MAD_WIDTH = 5.0
MAD_SCALE = 1.4826
THRESH = 3.0
LIMIT = 16 * 1024 * 1024

F32 = jnp.float32
BF16 = jnp.bfloat16


def iota(shape, axis):
    return lax.broadcasted_iota(jnp.int32, shape, axis)


def dot(a, b, dims=((1,), (0,))):
    return lax.dot_general(a, b, (dims, ((), ())), preferred_element_type=F32)


def split(value):
    high = value.astype(BF16).astype(F32)
    rest = value - high
    middle = rest.astype(BF16).astype(F32)
    return high, middle, rest - middle


def hit_ranks(marks, drifts, coarse):
    width = PER_COARSE * drifts
    row = jnp.zeros((coarse, width), F32)
    for b in range(PER_COARSE):
        pick = iota((coarse * PER_COARSE, coarse), 0) == iota(
            (coarse * PER_COARSE, coarse), 1
        ) * PER_COARSE + b
        of_block = dot(marks, jnp.where(pick, 1.0, 0.0).astype(BF16))
        place = iota((drifts, width), 1) == iota((drifts, width), 0) + b * drifts
        row += dot(of_block.astype(BF16), jnp.where(place, 1.0, 0.0).astype(BF16), ((0,), (0,)))
    order = lambda k: (k % drifts) * PER_COARSE + k // drifts
    before = order(iota((width, width), 0)) < order(iota((width, width), 1))
    rank = dot(row.astype(BF16), jnp.where(before, 1.0, 0.0).astype(BF16))
    return jnp.where(row > 0.5, rank, -1.0)


def pack_kernel(
    drifts, coarse, group,
    map_ref, median_ref, mad_ref, mask_hbm, spec_hbm, out_hbm,
    mask_ref, spec_ref, out_ref, rank_ref, key_ref, part_ref, extra_ref,
    mask_sem, spec_sem, out_sem, extra_sem,
):
    width = PER_COARSE * drifts
    span = group * COARSE_WIDTH
    fetch_mask = pltpu.make_async_copy(mask_hbm, mask_ref, mask_sem)
    fetch_mask.start()
    fetches = [
        pltpu.make_async_copy(
            spec_hbm.at[:, pl.ds(g * span, span)], spec_ref.at[:, pl.ds(g * span, span)], spec_sem.at[g]
        )
        for g in range(coarse // group)
    ]
    for fetch in fetches:
        fetch.start()
    fetch_mask.wait()
    rank_ref[...] = hit_ranks(mask_ref[...].astype(F32).astype(BF16), drifts, coarse)

    slots = iota((CAP, width), 0).astype(F32)
    position = iota((width, CAP), 0)
    label = ((position % drifts) * PER_COARSE + position // drifts + 1).astype(F32).astype(BF16)
    diagonal = iota((CAP, CAP), 0) == iota((CAP, CAP), 1)
    sends = []
    for at in range(coarse):
        if at % group == 0:
            fetches[at // group].wait()
        owner = lax.div(map_ref[at], coarse)
        chosen = jnp.where(rank_ref[at : at + 1, :] == slots, 1.0, 0.0).astype(BF16)
        base = at * COARSE_WIDTH
        blocks = [
            spec_ref[:, base + b * BLOCK : base + (b + 1) * BLOCK] for b in range(PER_COARSE)
        ]
        rows = jnp.concatenate(blocks, axis=0)
        taken = dot(chosen, jnp.concatenate([rows, label], axis=1))
        out_ref[at] = taken[:, :BLOCK].astype(BF16)
        send = pltpu.make_async_copy(
            out_ref.at[at], out_hbm.at[owner, pl.ds(0, CAP), :], out_sem.at[at]
        )
        send.start()
        sends.append(send)
        key_ref[pl.ds(owner, 1), :] = jnp.sum(
            jnp.where(diagonal, taken[:, BLOCK:], 0.0), axis=0, keepdims=True
        )
        center = BIN_STEP * median_ref[at].astype(F32)
        spread = MAD_WIDTH * BIN_STEP * mad_ref[at].astype(F32)
        low, high = center - spread, center + spread
        count = jnp.zeros((drifts, BLOCK), F32)
        first = jnp.zeros((drifts, BLOCK), F32)
        second = jnp.zeros((drifts, BLOCK), F32)
        for block in blocks:
            power = block.astype(F32)
            inside = (power >= low) & (power <= high)
            kept = jnp.where(inside, power - center, 0.0)
            count += jnp.where(inside, 1.0, 0.0)
            first += kept
            second += kept * kept
        for q, value in enumerate((count, first, second)):
            part_ref[q, pl.ds(owner, 1), :] = jnp.sum(value, axis=0, keepdims=True)
        fill = jnp.full((1, BLOCK), 1.0, F32)
        part_ref[3, pl.ds(owner, 1), :] = fill * center
        part_ref[4, pl.ds(owner, 1), :] = fill * mad_ref[at].astype(F32)

    lane = iota((coarse, BLOCK), 1)
    stats = jnp.zeros((coarse, BLOCK), F32)
    for q in range(3):
        for k, part in enumerate(split(jnp.sum(part_ref[q], axis=1, keepdims=True))):
            stats = jnp.where(lane == 3 * q + k, part, stats)
    for k, part in enumerate(split(part_ref[3])):
        stats = jnp.where(lane == 9 + k, part, stats)
    stats = jnp.where(lane == 12, part_ref[4], stats)
    line = iota((EXTRA, BLOCK), 0)
    for o in range(coarse):
        tile = jnp.where(
            line == 0, key_ref[o : o + 1, :], jnp.where(line == 1, stats[o : o + 1, :], 0.0)
        )
        extra_ref[o] = tile.astype(BF16)
    extra = pltpu.make_async_copy(extra_ref, out_hbm.at[:, pl.ds(CAP, EXTRA), :], extra_sem)
    extra.start()
    for send in sends:
        send.wait()
    extra.wait()


def pack(spectrum, hit_mask, owner_map, median_bin, mad_bin):
    drifts, channels = spectrum.shape
    coarse = owner_map.shape[0]
    group = 4
    smem = pl.BlockSpec(memory_space=pltpu.SMEM)
    hbm = pl.BlockSpec(memory_space=pl.ANY)
    return pl.pallas_call(
        functools.partial(pack_kernel, drifts, coarse, group),
        out_shape=jax.ShapeDtypeStruct((coarse, ROWS, BLOCK), BF16),
        in_specs=[smem, smem, smem, hbm, hbm],
        out_specs=hbm,
        scratch_shapes=[
            pltpu.VMEM((drifts, coarse * PER_COARSE), jnp.int32),
            pltpu.VMEM((drifts, channels), BF16),
            pltpu.VMEM((coarse, CAP, BLOCK), BF16),
            pltpu.VMEM((coarse, PER_COARSE * drifts), F32),
            pltpu.VMEM((coarse, CAP), F32),
            pltpu.VMEM((5, coarse, BLOCK), F32),
            pltpu.VMEM((coarse, EXTRA, BLOCK), BF16),
            pltpu.SemaphoreType.DMA,
            pltpu.SemaphoreType.DMA((coarse // group,)),
            pltpu.SemaphoreType.DMA((coarse,)),
            pltpu.SemaphoreType.DMA,
        ],
        name="pack",
    )(owner_map, median_bin, mad_bin, hit_mask, spectrum)


def unpack_kernel(
    senders, steps,
    at_ref, mine_ref, theirs_ref, rows_ref, snr_ref, key_ref, excess_ref, list_ref, keys_ref,
):
    step = pl.program_id(0)
    total = at_ref[senders]

    @pl.when(step == 0)
    def _():
        lane = iota((1, CAP), 1)
        half = at_ref[senders + 1]
        mine = mine_ref[...]
        both = mine + theirs_ref[...]
        floor_count = jnp.maximum(both[:, 0:1], 1.0)
        level = mine[:, 3:4] + both[:, 1:2] / floor_count
        mad_sigma = MAD_SCALE * BIN_STEP * mine[:, 4:5]
        sigma = jnp.sqrt(0.5 * both[:, 2:3] / floor_count + 0.5 * mad_sigma * mad_sigma)
        inverse = 1.0 / sigma
        for f in range(senders):
            start = at_ref[f]
            raw = rows_ref[f, :CAP, :].astype(F32)
            list_ref[pl.ds(start, CAP), :] = (raw - level[f : f + 1, :]) * inverse[f : f + 1, :]
            key = rows_ref[f, CAP : CAP + EXTRA, :].astype(F32)[0:1, :]
            key = key.astype(jnp.int32) + (f * 512 + half * 256 - 1)
            row = lax.div(start, CAP)
            shift = lax.rem(start, CAP)
            moved = pltpu.roll(key, shift, 1)
            keys_ref[pl.ds(row, 1), :] = jnp.where(
                lane >= shift, moved, keys_ref[pl.ds(row, 1), :]
            )
            keys_ref[pl.ds(row + 1, 1), :] = moved

    per = senders // steps
    ones = jnp.ones((2 * BLOCK, BLOCK), BF16)
    diagonal = iota((CAP, CAP), 0) == iota((CAP, CAP), 1)
    for j in range(per):
        row = step * per + j
        first = row * CAP
        block = list_ref[pl.ds(pl.multiple_of(first, CAP), CAP), :]
        live = iota((CAP, BLOCK), 0) + first < total
        value = jnp.where(live, block, 0.0).astype(BF16)
        snr_ref[0, 0, j * CAP : (j + 1) * CAP, :] = value
        over = jnp.maximum(value.astype(F32) - THRESH, 0.0)
        high = over.astype(BF16)
        low = (over - high.astype(F32)).astype(BF16)
        sums = dot(jnp.concatenate([high, low], axis=1), ones)
        excess_ref[pl.ds(row, 1), :] = jnp.sum(
            jnp.where(diagonal, sums, 0.0), axis=0, keepdims=True
        )
        key_ref[pl.ds(row, 1), :] = jnp.where(
            iota((1, CAP), 1) + first < total, keys_ref[pl.ds(row, 1), :], -1
        )


def unpack(at, mine, theirs, arrived):
    senders = arrived.shape[0]
    steps = 4
    total = senders * CAP
    return pl.pallas_call(
        functools.partial(unpack_kernel, senders, steps),
        out_shape=(
            jax.ShapeDtypeStruct((1, 1, total, BLOCK), BF16),
            jax.ShapeDtypeStruct((senders, CAP), jnp.int32),
            jax.ShapeDtypeStruct((senders, CAP), F32),
        ),
        grid_spec=pltpu.PrefetchScalarGridSpec(
            num_scalar_prefetch=1,
            grid=(steps,),
            in_specs=[
                pl.BlockSpec((senders, BLOCK), lambda i, m: (0, 0)),
                pl.BlockSpec((senders, BLOCK), lambda i, m: (0, 0)),
                pl.BlockSpec((senders, ROWS, BLOCK), lambda i, m: (0, 0, 0)),
            ],
            out_specs=[
                pl.BlockSpec((1, 1, total // steps, BLOCK), lambda i, m: (0, 0, i, 0)),
                pl.BlockSpec((senders, CAP), lambda i, m: (0, 0)),
                pl.BlockSpec((senders, CAP), lambda i, m: (0, 0)),
            ],
            scratch_shapes=[
                pltpu.VMEM((total, BLOCK), F32),
                pltpu.VMEM((senders + 8, CAP), jnp.int32),
            ],
        ),
        compiler_params=pltpu.CompilerParams(vmem_limit_bytes=LIMIT),
        name="unpack",
    )(at, mine, theirs, arrived)


def from_partner(value):
    pairs = lax.axis_size("sub")
    return lax.ppermute(value, "sub", [(i, (i + 1) % pairs) for i in range(pairs)])


def per_device(spectrum, hit_mask, owner_map, median_bin, mad_bin):
    senders = lax.axis_size("freq")
    payload = pack(spectrum, hit_mask, owner_map, median_bin, mad_bin)
    arrived = lax.all_to_all(payload, "freq", 0, 0, tiled=True)
    parts = arrived[:, CAP + 1, :].astype(F32)
    sums = [parts[:, 3 * q] + parts[:, 3 * q + 1] + parts[:, 3 * q + 2] for q in range(4)]
    mine = jnp.stack([*sums, parts[:, 12]], axis=1)
    mine = jnp.pad(mine, ((0, 0), (0, BLOCK - mine.shape[1])))
    theirs = from_partner(mine)
    got = jnp.sum((arrived[:, CAP, :].astype(F32) > 0.5).astype(jnp.int32), axis=1)
    rank = jnp.arange(senders, dtype=jnp.int32)
    starts = jnp.sum(jnp.where(rank[None, :] < rank[:, None], got[None, :], 0), axis=1)
    half = lax.axis_index("sub").astype(jnp.int32)
    at = jnp.concatenate([starts, jnp.stack([jnp.sum(got), half])])
    snr, keys, excess = unpack(at, mine, theirs, arrived)
    total = senders * CAP
    return snr, keys.reshape(1, 1, total), excess.reshape(1, 1, total)


def solution(mesh):
    placed = (
        P("sub", ("beam", "freq")),
        P("sub", ("beam", "freq")),
        P(("beam", "freq")),
        P(("beam", "freq")),
        P(("beam", "freq")),
    )
    return jax.shard_map(
        per_device,
        mesh=mesh,
        in_specs=placed,
        out_specs=(
            P("freq", "sub", "beam", None),
            P("freq", "sub", "beam"),
            P("freq", "sub", "beam"),
        ),
        check_vma=False,
    )
```

time: 185 us -> 158 us (0.85)
  blocking collectives: 55.2 us -> 0 us
  starting transfers between devices: 4.99 us -> 32.8 us
  other arithmetic: 5.45 us -> 2.17 us
  local copies, waits for them, and re-layouts: 3.34 us -> 0.09 us
  waiting for transfers between devices: 107 us -> 110 us
  Pallas kernels: 7.61 us -> 10.4 us
    all_to_all x1 -> x0, blocking collectives: 55.2 us -> none  [per_device(): lax.all_to_all(jnp.stack([labels, stats], axis=1), 'freq', 0, 0, tiled=True)]
    all_to_all x1, starting transfers between devices: 4.85 us -> 32.7 us  [per_device(): arrived = lax.all_to_all(payload, 'freq', 0, 0, tiled=True)]
    all_to_all x1, waiting for transfers between devices: 106 us -> 110 us  [per_device(): arrived = lax.all_to_all(payload, 'freq', 0, 0, tiled=True)]
    unnamed x19 -> x0, local copies, waits for them, and re-layouts: 3.26 us -> none
    pallas_call x1, Pallas kernels: 4.43 us -> 7.11 us  [pack(): pl.pallas_call(functools.partial(pack_kernel, drifts, coarse, group), out...]
    reduce_sum x6 -> x1, other arithmetic: 3.71 us -> 1.2 us  [per_device(): jnp.sum((arrived[:, CAP, :].astype(F32) > 0.5).astype(jnp.int32), axis=1)]
  transfers between devices with their start and end apart: 2 -> 2, of which waited for: 2 -> 1; matrix products, arithmetic and copies ran while one was open for 1% -> 1% of each run, Pallas kernels for 0% -> 0%
where the time goes in v2:
time: 158 us; the launch traced here: 156 us
  waiting for transfers between devices  110 us (70%)
  starting transfers between devices  32.8 us (21%)
  Pallas kernels  10.4 us (7%)
  other arithmetic  2.17 us (1%)
    all_to_all x1, waiting for transfers between devices, per_device(): arrived = lax.all_to_all(payload, 'freq', 0, 0, tiled=True)  110 us
    all_to_all x1, starting transfers between devices, per_device(): arrived = lax.all_to_all(payload, 'freq', 0, 0, tiled=True)  32.7 us
    pallas_call x1, Pallas kernels, pack(): pl.pallas_call(functools.partial(pack_kernel, drifts, coarse, group), out...  7.11 us
    pallas_call x1, Pallas kernels, unpack(): pl.pallas_call(functools.partial(unpack_kernel, senders, steps), out_shap...  3.28 us
  transfers between devices with their start and end apart: 2, of which 1 were waited for; matrix products, arithmetic and copies ran while one was open for 1% of the time, Pallas kernels for 0%

profile of v2, /device:TPU:46, one launch (start us, length us, event | category | flops | bytes accessed | tf_op | source)
XLA Modules:
  0.0 156.0 jit_solution(12271334450877566237)
XLA Ops:
  0.6 7.1 %pack.1 = bf16[32,136,128]{2,1,0:T(8,128)(2,1)} custom-call(s32[32]{0:T(128)} %map_ref.1, s32[32]{0:T(128)} %median_ref.1, s32[32]{0:T(128)} %mad_ref.1, s32[32,256]{1,0:T(8,128)} %mask_hbm.1, bf16[32,32768]{1,0:T(8,128)(2,1)} %spec_hbm.1), custom_call_target="tpu_custom_call" | custom-call | tf_op jit(solution)/shard_map/pack/pallas_call | solution.py:150
  7.7 32.7 %all-to-all-start = ((bf16[32,136,128]{2,1,0:T(8,128)(2,1)}), bf16[32,136,128]{2,1,0:T(8,128)(2,1)S(1)}, u32[]{:S(2)}, u32[]{:S(2)}) async-start(bf16[32,136,128]{2,1,0:T(8,128)(2,1)} %pack.1), calls=%async_computation | async-start | bytes 2228224 | tf_op jit(solution)/shard_map/all_to_all | solution.py:268
  40.4 109.9 %all-to-all-done.rows_ref = bf16[32,136,128]{2,1,0:T(8,128)(2,1)S(1)} async-done(((bf16[32,136,128]{2,1,0:T(8,128)(2,1)}), bf16[32,136,128]{2,1,0:T(8,128)(2,1)S(1)}, u32[]{:S(2)}, u32[]{:S(2)}) %all-to-all-start) | async-done | bytes 1114144 | tf_op jit(solution)/shard_map/all_to_all | solution.py:268
  150.3 0.1 fusion.2
  150.5 0.1 stack.15
  150.6 0.1 collective-permute-start
  150.7 1.2 fusion.1
  151.9 0.1 select_reduce_fusion
  152.0 0.7 pad_add_fusion.at_ref
  152.8 0.0 collective-permute-done.theirs_ref
  152.8 3.3 %unpack.1 = (bf16[1,1,4096,128]{3,2,1,0:T(8,128)(2,1)}, s32[32,128]{1,0:T(8,128)}, f32[32,128]{1,0:T(8,128)}) custom-call(s32[34]{0:T(128)S(1)} %pad_add_fusion.at_ref, f32[32,128]{1,0:T(8,128)S(1)} %pad.4.mine_ref, f32[32,128]{1,0:T(8,128)S(1)} %collective-permute-done.theirs_ref, bf16[32,136,128]{2,1,0:T(8,128)(2,1)S(1)} %all-to-all-done.rows_ref), custom_call_target="tpu_custom_call" | custom-call | tf_op jit(solution)/shard_map/unpack/pallas_call | solution.py:230
  (2 shorter events, 0.0 us)
Async XLA Ops:
  7.7 142.6 %all-to-all-start = ((bf16[32,136,128]{2,1,0:T(8,128)(2,1)}), bf16[32,136,128]{2,1,0:T(8,128)(2,1)S(1)}, u32[]{:S(2)}, u32[]{:S(2)}) async-start(bf16[32,136,128]{2,1,0:T(8,128)(2,1)} %pack.1), calls=%async_computation | async-start | bytes 2228224 | tf_op jit(solution)/shard_map/all_to_all | solution.py:268
  150.6 2.2 %collective-permute-start = (f32[32,128]{1,0:T(8,128)S(1)}, f32[32,128]{1,0:T(8,128)S(1)}, u32[]{:S(2)}, u32[]{:S(2)}) collective-permute-start(f32[32,128]{1,0:T(8,128)S(1)} %pad.4.mine_ref), channel_id=1, source_target_pairs={{0,1},{1,0},{2,3},{3,2},{4,5},{5,4},{6,7},{7,6},{8,9},{9,8},{10,11... | collective-permute-start | bytes 49160 | tf_op jit(solution)/shard_map/ppermute | solution.py:262

commit v3 on v2

v3 whole, which is shorter than its diff:
```python
import functools

import jax
import jax.numpy as jnp
from jax import lax
from jax.experimental import pallas as pl
from jax.experimental.pallas import tpu as pltpu
from jax.sharding import PartitionSpec as P

COARSE_WIDTH = 1024
BLOCK = 128
CAP = 128
PER_COARSE = COARSE_WIDTH // BLOCK
EXTRA = 2
ROWS = CAP + EXTRA

BIN_STEP = 0.0625
MAD_WIDTH = 5.0
MAD_SCALE = 1.4826
THRESH = 3.0
LIMIT = 16 * 1024 * 1024

F32 = jnp.float32
BF16 = jnp.bfloat16


def iota(shape, axis):
    return lax.broadcasted_iota(jnp.int32, shape, axis)


def dot(a, b, dims=((1,), (0,))):
    return lax.dot_general(a, b, (dims, ((), ())), preferred_element_type=F32)


def split(value):
    high = value.astype(BF16).astype(F32)
    rest = value - high
    middle = rest.astype(BF16).astype(F32)
    return high, middle, rest - middle


def hit_ranks(marks, drifts, coarse):
    width = PER_COARSE * drifts
    row = jnp.zeros((coarse, width), F32)
    for b in range(PER_COARSE):
        pick = iota((coarse * PER_COARSE, coarse), 0) == iota(
            (coarse * PER_COARSE, coarse), 1
        ) * PER_COARSE + b
        of_block = dot(marks, jnp.where(pick, 1.0, 0.0).astype(BF16))
        place = iota((drifts, width), 1) == iota((drifts, width), 0) + b * drifts
        row += dot(of_block.astype(BF16), jnp.where(place, 1.0, 0.0).astype(BF16), ((0,), (0,)))
    order = lambda k: (k % drifts) * PER_COARSE + k // drifts
    before = order(iota((width, width), 0)) < order(iota((width, width), 1))
    rank = dot(row.astype(BF16), jnp.where(before, 1.0, 0.0).astype(BF16))
    return jnp.where(row > 0.5, rank, -1.0)


def pack_kernel(
    drifts, coarse, group,
    map_ref, median_ref, mad_ref, mask_hbm, spec_hbm, out_hbm,
    mask_ref, spec_ref, out_ref, rank_ref, key_ref, part_ref, from_ref,
    mask_sem, spec_sem, out_sem,
):
    width = PER_COARSE * drifts
    fetch_mask = pltpu.make_async_copy(mask_hbm, mask_ref, mask_sem)
    fetch_mask.start()
    fetch = pltpu.make_async_copy(spec_hbm, spec_ref, spec_sem)
    fetch.start()
    for c in range(coarse):
        from_ref[lax.div(map_ref[c], coarse)] = c
    fetch_mask.wait()
    rank_ref[...] = hit_ranks(mask_ref[...].astype(F32).astype(BF16), drifts, coarse)

    slots = iota((CAP, width), 0).astype(F32)
    position = iota((width, CAP), 0)
    label = ((position % drifts) * PER_COARSE + position // drifts + 1).astype(F32).astype(BF16)
    diagonal = iota((CAP, CAP), 0) == iota((CAP, CAP), 1)
    lane = iota((group, BLOCK), 1)
    line = iota((EXTRA, BLOCK), 0)
    fetch.wait()
    sends = []
    for owner in range(coarse):
        c = from_ref[owner]
        chosen = jnp.where(rank_ref[pl.ds(c, 1), :] == slots, 1.0, 0.0).astype(BF16)
        blocks = [
            spec_ref[:, pl.ds(pl.multiple_of(c * COARSE_WIDTH + b * BLOCK, BLOCK), BLOCK)]
            for b in range(PER_COARSE)
        ]
        rows = jnp.concatenate(blocks, axis=0)
        taken = dot(chosen, jnp.concatenate([rows, label], axis=1))
        base = owner * ROWS
        out_ref[base : base + CAP, :] = taken[:, :BLOCK].astype(BF16)
        mine = owner % group
        key_ref[mine : mine + 1, :] = jnp.sum(
            jnp.where(diagonal, taken[:, BLOCK:], 0.0), axis=0, keepdims=True
        )
        mad = mad_ref[c].astype(F32)
        center = BIN_STEP * median_ref[c].astype(F32)
        spread = MAD_WIDTH * BIN_STEP * mad
        low, high = center - spread, center + spread
        count = jnp.zeros((drifts, BLOCK), F32)
        first = jnp.zeros((drifts, BLOCK), F32)
        second = jnp.zeros((drifts, BLOCK), F32)
        for block in blocks:
            power = block.astype(F32)
            inside = (power >= low) & (power <= high)
            kept = jnp.where(inside, power - center, 0.0)
            count += jnp.where(inside, 1.0, 0.0)
            first += kept
            second += kept * kept
        for q, value in enumerate((count, first, second)):
            part_ref[q, mine : mine + 1, :] = jnp.sum(value, axis=0, keepdims=True)
        part_ref[3, mine : mine + 1, :] = jnp.full((1, BLOCK), center, F32)
        part_ref[4, mine : mine + 1, :] = jnp.full((1, BLOCK), mad, F32)
        if mine + 1 < group:
            continue
        stats = jnp.where(lane == 12, part_ref[4], 0.0)
        for q in range(4):
            whole = jnp.sum(part_ref[q], axis=1, keepdims=True) if q < 3 else part_ref[q]
            for k, part in enumerate(split(whole)):
                stats = jnp.where(lane == 3 * q + k, part, stats)
        for k in range(group):
            tail = (owner - mine + k) * ROWS + CAP
            both = jnp.where(line == 0, key_ref[k : k + 1, :], stats[k : k + 1, :])
            out_ref[tail : tail + EXTRA, :] = both.astype(BF16)
        part = pl.ds((owner - mine) * ROWS, group * ROWS)
        send = pltpu.make_async_copy(
            out_ref.at[part, :], out_hbm.at[part, :], out_sem.at[owner // group]
        )
        send.start()
        sends.append(send)
    for send in sends:
        send.wait()


def pack(spectrum, hit_mask, owner_map, median_bin, mad_bin):
    drifts, channels = spectrum.shape
    coarse = owner_map.shape[0]
    group = 8
    smem = pl.BlockSpec(memory_space=pltpu.SMEM)
    hbm = pl.BlockSpec(memory_space=pl.ANY)
    return pl.pallas_call(
        functools.partial(pack_kernel, drifts, coarse, group),
        out_shape=jax.ShapeDtypeStruct((coarse * ROWS, BLOCK), BF16),
        in_specs=[smem, smem, smem, hbm, hbm],
        out_specs=hbm,
        scratch_shapes=[
            pltpu.VMEM((drifts, coarse * PER_COARSE), jnp.int32),
            pltpu.VMEM((drifts, channels), BF16),
            pltpu.VMEM((coarse * ROWS, BLOCK), BF16),
            pltpu.VMEM((coarse, PER_COARSE * drifts), F32),
            pltpu.VMEM((group, CAP), F32),
            pltpu.VMEM((5, group, BLOCK), F32),
            pltpu.SMEM((coarse,), jnp.int32),
            pltpu.SemaphoreType.DMA,
            pltpu.SemaphoreType.DMA,
            pltpu.SemaphoreType.DMA((coarse // group,)),
        ],
        name="pack",
    )(owner_map, median_bin, mad_bin, hit_mask, spectrum)


def unpack_kernel(
    senders, steps,
    half_ref, mine_ref, theirs_ref, rows_ref, snr_ref, key_ref, excess_ref,
    list_ref, keys_ref, label_ref, total_ref,
):
    step = pl.program_id(0)

    @pl.when(step == 0)
    def _():
        lane = iota((1, CAP), 1)
        half = half_ref[0]
        for f in range(senders):
            tail = f * ROWS + CAP
            label_ref[f : f + 1, :] = rows_ref[tail : tail + EXTRA, :].astype(F32)[0:1, :]
        label = label_ref[...]
        filled = jnp.sum(jnp.where(label > 0.5, 1.0, 0.0), axis=1, keepdims=True)
        before = iota((senders, senders), 1) < iota((senders, senders), 0)
        starts = dot(
            jnp.where(before, 1.0, 0.0).astype(BF16),
            jnp.broadcast_to(filled, (senders, BLOCK)).astype(BF16),
        ).astype(jnp.int32)
        total_ref[0] = starts[senders - 1, 0] + filled.astype(jnp.int32)[senders - 1, 0]
        mine = mine_ref[...]
        both = mine + theirs_ref[...]
        floor_count = jnp.maximum(both[:, 0:1], 1.0)
        level = mine[:, 3:4] + both[:, 1:2] / floor_count
        mad_sigma = MAD_SCALE * BIN_STEP * mine[:, 4:5]
        sigma = jnp.sqrt(0.5 * both[:, 2:3] / floor_count + 0.5 * mad_sigma * mad_sigma)
        inverse = 1.0 / sigma
        for f in range(senders):
            start = starts[f, 0]
            raw = rows_ref[f * ROWS : f * ROWS + CAP, :].astype(F32)
            list_ref[pl.ds(start, CAP), :] = (raw - level[f : f + 1, :]) * inverse[f : f + 1, :]
            key = label[f : f + 1, :].astype(jnp.int32) + (f * 512 + half * 256 - 1)
            row = lax.div(start, CAP)
            shift = lax.rem(start, CAP)
            moved = pltpu.roll(key, shift, 1)
            keys_ref[pl.ds(row, 1), :] = jnp.where(
                lane >= shift, moved, keys_ref[pl.ds(row, 1), :]
            )
            keys_ref[pl.ds(row + 1, 1), :] = moved

    total = total_ref[0]
    per = senders // steps
    ones = jnp.ones((2 * BLOCK, BLOCK), BF16)
    diagonal = iota((CAP, CAP), 0) == iota((CAP, CAP), 1)
    for j in range(per):
        row = step * per + j
        first = row * CAP
        block = list_ref[pl.ds(pl.multiple_of(first, CAP), CAP), :]
        live = iota((CAP, BLOCK), 0) + first < total
        value = jnp.where(live, block, 0.0).astype(BF16)
        snr_ref[0, 0, j * CAP : (j + 1) * CAP, :] = value
        over = jnp.maximum(value.astype(F32) - THRESH, 0.0)
        high = over.astype(BF16)
        low = (over - high.astype(F32)).astype(BF16)
        sums = dot(jnp.concatenate([high, low], axis=1), ones)
        excess_ref[pl.ds(row, 1), :] = jnp.sum(
            jnp.where(diagonal, sums, 0.0), axis=0, keepdims=True
        )
        key_ref[pl.ds(row, 1), :] = jnp.where(
            iota((1, CAP), 1) + first < total, keys_ref[pl.ds(row, 1), :], -1
        )


def unpack(half, mine, theirs, arrived):
    senders = mine.shape[0]
    steps = 4
    total = senders * CAP
    return pl.pallas_call(
        functools.partial(unpack_kernel, senders, steps),
        out_shape=(
            jax.ShapeDtypeStruct((1, 1, total, BLOCK), BF16),
            jax.ShapeDtypeStruct((senders, CAP), jnp.int32),
            jax.ShapeDtypeStruct((senders, CAP), F32),
        ),
        grid_spec=pltpu.PrefetchScalarGridSpec(
            num_scalar_prefetch=1,
            grid=(steps,),
            in_specs=[
                pl.BlockSpec((senders, BLOCK), lambda i, m: (0, 0)),
                pl.BlockSpec((senders, BLOCK), lambda i, m: (0, 0)),
                pl.BlockSpec((senders * ROWS, BLOCK), lambda i, m: (0, 0)),
            ],
            out_specs=[
                pl.BlockSpec((1, 1, total // steps, BLOCK), lambda i, m: (0, 0, i, 0)),
                pl.BlockSpec((senders, CAP), lambda i, m: (0, 0)),
                pl.BlockSpec((senders, CAP), lambda i, m: (0, 0)),
            ],
            scratch_shapes=[
                pltpu.VMEM((total, BLOCK), F32),
                pltpu.VMEM((senders + 8, CAP), jnp.int32),
                pltpu.VMEM((senders, CAP), F32),
                pltpu.SMEM((1,), jnp.int32),
            ],
        ),
        compiler_params=pltpu.CompilerParams(vmem_limit_bytes=LIMIT),
        name="unpack",
    )(half, mine, theirs, arrived)


def from_partner(value):
    pairs = lax.axis_size("sub")
    return lax.ppermute(value, "sub", [(i, (i + 1) % pairs) for i in range(pairs)])


def per_device(spectrum, hit_mask, owner_map, median_bin, mad_bin):
    senders = lax.axis_size("freq")
    payload = pack(spectrum, hit_mask, owner_map, median_bin, mad_bin)
    pairs = payload.reshape(senders, ROWS // 2, 2, BLOCK)
    arrived = lax.all_to_all(pairs, "freq", 0, 0, tiled=True)
    parts = arrived[:, CAP // 2, 1, :].astype(F32)
    sums = [parts[:, 3 * q] + parts[:, 3 * q + 1] + parts[:, 3 * q + 2] for q in range(4)]
    mine = jnp.stack([*sums, parts[:, 12]], axis=1)
    mine = jnp.pad(mine, ((0, 0), (0, BLOCK - mine.shape[1])))
    half = lax.axis_index("sub").astype(jnp.int32)
    snr, keys, excess = unpack(
        half[None], mine, from_partner(mine), arrived.reshape(payload.shape)
    )
    total = senders * CAP
    return snr, keys.reshape(1, 1, total), excess.reshape(1, 1, total)


def solution(mesh):
    placed = (
        P("sub", ("beam", "freq")),
        P("sub", ("beam", "freq")),
        P(("beam", "freq")),
        P(("beam", "freq")),
        P(("beam", "freq")),
    )
    return jax.shard_map(
        per_device,
        mesh=mesh,
        in_specs=placed,
        out_specs=(
            P("freq", "sub", "beam", None),
            P("freq", "sub", "beam"),
            P("freq", "sub", "beam"),
        ),
        check_vma=False,
    )
```

time: 158 us -> 156 us (0.987)
  blocking collectives: 0 us -> 144 us
  waiting for transfers between devices: 110 us -> 1.15 us
  starting transfers between devices: 32.8 us -> 0.14 us
  other arithmetic: 2.17 us -> 0.12 us
  Pallas kernels: 10.4 us -> 8.82 us
    all_to_all x0 -> x1, blocking collectives: none -> 144 us  [per_device(): arrived = lax.all_to_all(pairs, 'freq', 0, 0, tiled=True)]
    all_to_all x1 -> x0, waiting for transfers between devices: 110 us -> none  [per_device(): arrived = lax.all_to_all(payload, 'freq', 0, 0, tiled=True)]
    all_to_all x1 -> x0, starting transfers between devices: 32.7 us -> none  [per_device(): arrived = lax.all_to_all(payload, 'freq', 0, 0, tiled=True)]
  transfers between devices with their start and end apart: 2 -> 1, of which waited for: 1 -> 1; matrix products, arithmetic and copies ran while one was open for 1% -> 0% of each run, Pallas kernels for 0% -> 0%
where the time goes in v3:
time: 156 us; the launch traced here: 155 us
  blocking collectives  144 us (92%)
  Pallas kernels  8.82 us (6%)
    all_to_all x1, blocking collectives, per_device(): arrived = lax.all_to_all(pairs, 'freq', 0, 0, tiled=True)  144 us
    pallas_call x1, Pallas kernels, pack(): pl.pallas_call(functools.partial(pack_kernel, drifts, coarse, group), out...  5.95 us
  transfers between devices with their start and end apart: 1, of which 1 were waited for; matrix products, arithmetic and copies ran while one was open for 0% of the time, Pallas kernels for 0%

profile of v3, /device:TPU:46, one launch (start us, length us, event | category | flops | bytes accessed | tf_op | source)
XLA Modules:
  0.0 154.7 jit_solution(15640568220286277323)
XLA Ops:
  0.6 6.0 %pack.1 = bf16[4160,128]{1,0:T(8,128)(2,1)} custom-call(s32[32]{0:T(128)} %map_ref.1, s32[32]{0:T(128)} %median_ref.1, s32[32]{0:T(128)} %mad_ref.1, s32[32,256]{1,0:T(8,128)} %mask_hbm.1, bf16[32,32768]{1,0:T(8,128)(2,1)} %spec_hbm.1), custom_call_target="tpu_custom_call" | custom-call | tf_op jit(solution)/shard_map/pack/pallas_call | solution.py:142
  6.6 143.7 %all_to_all.5 = bf16[32,65,2,128]{3,2,1,0:T(2,128)(2,1)S(1)} all-to-all(bf16[32,65,2,128]{3,2,1,0:T(2,128)(2,1)} %bitcast.11), channel_id=1, replica_groups=mesh['beam'=4,'freq'=32,'sub'=2] {'freq'}, dimensions={0} | all-to-all | bytes 2129920 | tf_op jit(solution)/shard_map/all_to_all | solution.py:273
  150.3 0.1 fusion.1
  150.4 0.1 stack.2
  150.5 0.1 collective-permute-start
  150.7 1.2 collective-permute-done.theirs_ref
  151.8 2.9 %unpack.1 = (bf16[1,1,4096,128]{3,2,1,0:T(8,128)(2,1)}, s32[32,128]{1,0:T(8,128)}, f32[32,128]{1,0:T(8,128)}) custom-call(s32[1]{0:T(128)} %bitcast.half_ref, f32[32,128]{1,0:T(8,128)S(1)} %pad.4.mine_ref, f32[32,128]{1,0:T(8,128)S(1)} %collective-permute-done.theirs_ref, bf16[4160,128]{1,0:T(8,128)(2,1)S(1)} %bitcast.10), custom_call_target="tpu_custom_call" | custom-call | tf_op jit(solution)/shard_map/unpack/pallas_call | solution.py:232
  (3 shorter events, 0.0 us)
Async XLA Ops:
  150.5 1.3 collective-permute-start

commit v4 on v3

--- a/solution.py
+++ b/solution.py
@@ -57,15 +57,25 @@
 
 def pack_kernel(
     drifts, coarse, group,
-    map_ref, median_ref, mad_ref, mask_hbm, spec_hbm, out_hbm,
-    mask_ref, spec_ref, out_ref, rank_ref, key_ref, part_ref, from_ref,
-    mask_sem, spec_sem, out_sem,
+    map_hbm, median_hbm, mad_hbm, mask_hbm, spec_hbm, out_hbm,
+    mask_ref, spec_ref, out_ref, rank_ref, key_ref, part_ref, from_ref, map_ref, median_ref, mad_ref,
+    mask_sem, spec_sem, out_sem, small_sem,
 ):
     width = PER_COARSE * drifts
+    small = [
+        pltpu.make_async_copy(source, target, small_sem.at[i])
+        for i, (source, target) in enumerate(
+            [(map_hbm, map_ref), (median_hbm, median_ref), (mad_hbm, mad_ref)]
+        )
+    ]
+    for copy in small:
+        copy.start()
     fetch_mask = pltpu.make_async_copy(mask_hbm, mask_ref, mask_sem)
     fetch_mask.start()
     fetch = pltpu.make_async_copy(spec_hbm, spec_ref, spec_sem)
     fetch.start()
+    for copy in small:
+        copy.wait()
     for c in range(coarse):
         from_ref[lax.div(map_ref[c], coarse)] = c
     fetch_mask.wait()
@@ -142,7 +152,7 @@
     return pl.pallas_call(
         functools.partial(pack_kernel, drifts, coarse, group),
         out_shape=jax.ShapeDtypeStruct((coarse * ROWS, BLOCK), BF16),
-        in_specs=[smem, smem, smem, hbm, hbm],
+        in_specs=[hbm] * 5,
         out_specs=hbm,
         scratch_shapes=[
             pltpu.VMEM((drifts, coarse * PER_COARSE), jnp.int32),
@@ -152,113 +162,115 @@
             pltpu.VMEM((group, CAP), F32),
             pltpu.VMEM((5, group, BLOCK), F32),
             pltpu.SMEM((coarse,), jnp.int32),
+            pltpu.SMEM((coarse,), jnp.int32),
+            pltpu.SMEM((coarse,), jnp.int32),
+            pltpu.SMEM((coarse,), jnp.int32),
             pltpu.SemaphoreType.DMA,
             pltpu.SemaphoreType.DMA,
             pltpu.SemaphoreType.DMA((coarse // group,)),
+            pltpu.SemaphoreType.DMA((3,)),
         ],
         name="pack",
     )(owner_map, median_bin, mad_bin, hit_mask, spectrum)
 
 
 def unpack_kernel(
-    senders, steps,
-    half_ref, mine_ref, theirs_ref, rows_ref, snr_ref, key_ref, excess_ref,
-    list_ref, keys_ref, label_ref, total_ref,
+    senders, part,
+    mine_ref, theirs_ref, rows_ref, snr_hbm, key_hbm, excess_hbm,
+    list_ref, snr_ref, keys_ref, excess_ref, label_ref, snr_sem, key_sem, excess_sem,
 ):
-    step = pl.program_id(0)
-
-    @pl.when(step == 0)
-    def _():
-        lane = iota((1, CAP), 1)
-        half = half_ref[0]
-        for f in range(senders):
-            tail = f * ROWS + CAP
-            label_ref[f : f + 1, :] = rows_ref[tail : tail + EXTRA, :].astype(F32)[0:1, :]
-        label = label_ref[...]
-        filled = jnp.sum(jnp.where(label > 0.5, 1.0, 0.0), axis=1, keepdims=True)
-        before = iota((senders, senders), 1) < iota((senders, senders), 0)
-        starts = dot(
-            jnp.where(before, 1.0, 0.0).astype(BF16),
-            jnp.broadcast_to(filled, (senders, BLOCK)).astype(BF16),
-        ).astype(jnp.int32)
-        total_ref[0] = starts[senders - 1, 0] + filled.astype(jnp.int32)[senders - 1, 0]
-        mine = mine_ref[...]
-        both = mine + theirs_ref[...]
-        floor_count = jnp.maximum(both[:, 0:1], 1.0)
-        level = mine[:, 3:4] + both[:, 1:2] / floor_count
-        mad_sigma = MAD_SCALE * BIN_STEP * mine[:, 4:5]
-        sigma = jnp.sqrt(0.5 * both[:, 2:3] / floor_count + 0.5 * mad_sigma * mad_sigma)
-        inverse = 1.0 / sigma
-        for f in range(senders):
-            start = starts[f, 0]
-            raw = rows_ref[f * ROWS : f * ROWS + CAP, :].astype(F32)
-            list_ref[pl.ds(start, CAP), :] = (raw - level[f : f + 1, :]) * inverse[f : f + 1, :]
-            key = label[f : f + 1, :].astype(jnp.int32) + (f * 512 + half * 256 - 1)
-            row = lax.div(start, CAP)
-            shift = lax.rem(start, CAP)
-            moved = pltpu.roll(key, shift, 1)
-            keys_ref[pl.ds(row, 1), :] = jnp.where(
-                lane >= shift, moved, keys_ref[pl.ds(row, 1), :]
-            )
-            keys_ref[pl.ds(row + 1, 1), :] = moved
-
-    total = total_ref[0]
-    per = senders // steps
+    lane = iota((1, CAP), 1)
+    half = lax.axis_index("sub")
+    for f in range(senders):
+        tail = f * ROWS + CAP
+        label_ref[f : f + 1, :] = rows_ref[tail : tail + EXTRA, :].astype(F32)[0:1, :]
+    label = label_ref[...]
+    filled = jnp.sum(jnp.where(label > 0.5, 1.0, 0.0), axis=1, keepdims=True)
+    before = iota((senders, senders), 1) < iota((senders, senders), 0)
+    starts = dot(
+        jnp.where(before, 1.0, 0.0).astype(BF16),
+        jnp.broadcast_to(filled, (senders, BLOCK)).astype(BF16),
+    ).astype(jnp.int32)
+    total = starts[senders - 1, 0] + filled.astype(jnp.int32)[senders - 1, 0]
+    mine, theirs = mine_ref[...].astype(F32), theirs_ref[...].astype(F32)
+    whole = lambda v, q: sum(v[:, 3 * q + k : 3 * q + k + 1] for k in range(3))
+    count, first, second = (whole(mine, q) + whole(theirs, q) for q in range(3))
+    floor_count = jnp.maximum(count, 1.0)
+    level = whole(mine, 3) + first / floor_count
+    mad_sigma = MAD_SCALE * BIN_STEP * mine[:, 12:13]
+    sigma = jnp.sqrt(0.5 * second / floor_count + 0.5 * mad_sigma * mad_sigma)
+    inverse = 1.0 / sigma
+    for f in range(senders):
+        start = starts[f, 0]
+        raw = rows_ref[f * ROWS : f * ROWS + CAP, :].astype(F32)
+        list_ref[pl.ds(start, CAP), :] = (raw - level[f : f + 1, :]) * inverse[f : f + 1, :]
+        key = label[f : f + 1, :].astype(jnp.int32) + (f * 512 + half * 256 - 1)
+        row = lax.div(start, CAP)
+        shift = lax.rem(start, CAP)
+        moved = pltpu.roll(key, shift, 1)
+        keys_ref[pl.ds(row, 1), :] = jnp.where(lane >= shift, moved, keys_ref[pl.ds(row, 1), :])
+        keys_ref[pl.ds(row + 1, 1), :] = moved
+    place = iota((senders, CAP), 0) * CAP + iota((senders, CAP), 1)
+    keys_ref[:senders, :] = jnp.where(place < total, keys_ref[:senders, :], -1)
+    copies = [pltpu.make_async_copy(keys_ref.at[pl.ds(0, senders), :], key_hbm, key_sem)]
+    copies[0].start()
+
     ones = jnp.ones((2 * BLOCK, BLOCK), BF16)
     diagonal = iota((CAP, CAP), 0) == iota((CAP, CAP), 1)
-    for j in range(per):
-        row = step * per + j
-        first = row * CAP
-        block = list_ref[pl.ds(pl.multiple_of(first, CAP), CAP), :]
-        live = iota((CAP, BLOCK), 0) + first < total
-        value = jnp.where(live, block, 0.0).astype(BF16)
-        snr_ref[0, 0, j * CAP : (j + 1) * CAP, :] = value
+    for row in range(senders):
+        at = slice(row * CAP, (row + 1) * CAP)
+        live = iota((CAP, BLOCK), 0) < total - row * CAP
+        value = jnp.where(live, list_ref[at, :], 0.0).astype(BF16)
+        snr_ref[at, :] = value
+        if row % part == part - 1:
+            done = pl.ds((row + 1 - part) * CAP, part * CAP)
+            copies.append(
+                pltpu.make_async_copy(
+                    snr_ref.at[done, :], snr_hbm.at[0, 0, done, :], snr_sem.at[row // part]
+                )
+            )
+            copies[-1].start()
         over = jnp.maximum(value.astype(F32) - THRESH, 0.0)
         high = over.astype(BF16)
         low = (over - high.astype(F32)).astype(BF16)
         sums = dot(jnp.concatenate([high, low], axis=1), ones)
-        excess_ref[pl.ds(row, 1), :] = jnp.sum(
+        excess_ref[row : row + 1, :] = jnp.sum(
             jnp.where(diagonal, sums, 0.0), axis=0, keepdims=True
         )
-        key_ref[pl.ds(row, 1), :] = jnp.where(
-            iota((1, CAP), 1) + first < total, keys_ref[pl.ds(row, 1), :], -1
-        )
-
-
-def unpack(half, mine, theirs, arrived):
+    copies.append(pltpu.make_async_copy(excess_ref, excess_hbm, excess_sem))
+    copies[-1].start()
+    for copy in copies:
+        copy.wait()
+
+
+def unpack(mine, theirs, arrived):
     senders = mine.shape[0]
-    steps = 4
+    part = 4
     total = senders * CAP
+    vmem = pl.BlockSpec(memory_space=pltpu.VMEM)
+    hbm = pl.BlockSpec(memory_space=pl.ANY)
     return pl.pallas_call(
-        functools.partial(unpack_kernel, senders, steps),
+        functools.partial(unpack_kernel, senders, part),
         out_shape=(
             jax.ShapeDtypeStruct((1, 1, total, BLOCK), BF16),
             jax.ShapeDtypeStruct((senders, CAP), jnp.int32),
             jax.ShapeDtypeStruct((senders, CAP), F32),
         ),
-        grid_spec=pltpu.PrefetchScalarGridSpec(
-            num_scalar_prefetch=1,
-            grid=(steps,),
-            in_specs=[
-                pl.BlockSpec((senders, BLOCK), lambda i, m: (0, 0)),
-                pl.BlockSpec((senders, BLOCK), lambda i, m: (0, 0)),
-                pl.BlockSpec((senders * ROWS, BLOCK), lambda i, m: (0, 0)),
-            ],
-            out_specs=[
-                pl.BlockSpec((1, 1, total // steps, BLOCK), lambda i, m: (0, 0, i, 0)),
-                pl.BlockSpec((senders, CAP), lambda i, m: (0, 0)),
-                pl.BlockSpec((senders, CAP), lambda i, m: (0, 0)),
-            ],
-            scratch_shapes=[
-                pltpu.VMEM((total, BLOCK), F32),
-                pltpu.VMEM((senders + 8, CAP), jnp.int32),
-                pltpu.VMEM((senders, CAP), F32),
-                pltpu.SMEM((1,), jnp.int32),
-            ],
-        ),
+        in_specs=[vmem, vmem, vmem],
+        out_specs=[hbm, hbm, hbm],
+        scratch_shapes=[
+            pltpu.VMEM((total, BLOCK), F32),
+            pltpu.VMEM((total, BLOCK), BF16),
+            pltpu.VMEM((senders + 8, CAP), jnp.int32),
+            pltpu.VMEM((senders, CAP), F32),
+            pltpu.VMEM((senders, CAP), F32),
+            pltpu.SemaphoreType.DMA((senders // part,)),
+            pltpu.SemaphoreType.DMA,
+            pltpu.SemaphoreType.DMA,
+        ],
         compiler_params=pltpu.CompilerParams(vmem_limit_bytes=LIMIT),
         name="unpack",
-    )(half, mine, theirs, arrived)
+    )(mine, theirs, arrived)
 
 
 def from_partner(value):
@@ -271,14 +283,8 @@
     payload = pack(spectrum, hit_mask, owner_map, median_bin, mad_bin)
     pairs = payload.reshape(senders, ROWS // 2, 2, BLOCK)
     arrived = lax.all_to_all(pairs, "freq", 0, 0, tiled=True)
-    parts = arrived[:, CAP // 2, 1, :].astype(F32)
-    sums = [parts[:, 3 * q] + parts[:, 3 * q + 1] + parts[:, 3 * q + 2] for q in range(4)]
-    mine = jnp.stack([*sums, parts[:, 12]], axis=1)
-    mine = jnp.pad(mine, ((0, 0), (0, BLOCK - mine.shape[1])))
-    half = lax.axis_index("sub").astype(jnp.int32)
-    snr, keys, excess = unpack(
-        half[None], mine, from_partner(mine), arrived.reshape(payload.shape)
-    )
+    mine = arrived[:, CAP // 2, 1, :]
+    snr, keys, excess = unpack(mine, from_partner(mine), arrived.reshape(payload.shape))
     total = senders * CAP
     return snr, keys.reshape(1, 1, total), excess.reshape(1, 1, total)
 

time: 156 us -> 155 us (level)
  no operation moved by 1% of the time
where the time goes in v4:
time: 155 us; the launch traced here: 153 us
  blocking collectives  144 us (93%)
  Pallas kernels  7.65 us (5%)
    all_to_all x1, blocking collectives, per_device(): arrived = lax.all_to_all(pairs, 'freq', 0, 0, tiled=True)  144 us
    pallas_call x1, Pallas kernels, pack(): pl.pallas_call(functools.partial(pack_kernel, drifts, coarse, group), out...  5.31 us
  transfers between devices with their start and end apart: 1, of which 1 were waited for; matrix products, arithmetic and copies ran while one was open for 0% of the time, Pallas kernels for 0%

profile of v4, /device:TPU:46, one launch (start us, length us, event | category | flops | bytes accessed | tf_op | source)
XLA Modules:
  0.0 153.3 jit_solution(13466628619565926645)
XLA Ops:
  0.6 5.3 %pack.1 = bf16[4160,128]{1,0:T(8,128)(2,1)} custom-call(s32[32]{0:T(128)} %map_hbm.1, s32[32]{0:T(128)} %median_hbm.1, s32[32]{0:T(128)} %mad_hbm.1, s32[32,256]{1,0:T(8,128)} %mask_hbm.1, bf16[32,32768]{1,0:T(8,128)(2,1)} %spec_hbm.1), custom_call_target="tpu_custom_call" | custom-call | tf_op jit(solution)/shard_map/pack/pallas_call | solution.py:152
  6.0 143.7 %all_to_all.5 = bf16[32,65,2,128]{3,2,1,0:T(2,128)(2,1)S(1)} all-to-all(bf16[32,65,2,128]{3,2,1,0:T(2,128)(2,1)} %bitcast.10), channel_id=1, replica_groups=mesh['beam'=4,'freq'=32,'sub'=2] {'freq'}, dimensions={0} | all-to-all | bytes 2129920 | tf_op jit(solution)/shard_map/all_to_all | solution.py:285
  149.7 0.1 collective-permute-start
  149.8 1.1 collective-permute-done.theirs_ref
  151.0 2.3 %unpack.1 = (bf16[1,1,4096,128]{3,2,1,0:T(8,128)(2,1)}, s32[32,128]{1,0:T(8,128)}, f32[32,128]{1,0:T(8,128)}) custom-call(bf16[32,128]{1,0:T(8,128)(2,1)S(1)} %bitcast.9, bf16[32,128]{1,0:T(8,128)(2,1)S(1)} %collective-permute-done.theirs_ref, bf16[4160,128]{1,0:T(8,128)(2,1)S(1)} %bitcast.7), custom_call_target="tpu_custom_call" | custom-call | tf_op jit(solution)/shard_map/unpack/pallas_call | solution.py:252
  (2 shorter events, 0.0 us)
Async XLA Ops:
  149.7 1.3 collective-permute-start
